TPU v7x, 32 devices: a whole 2x2x4 slice. The times are simulated.
32 devices in a mesh: chan: 4 (over z), tm: 8 (over y, x, core).
Axes of the slice: x: 2, y: 2, z: 4, core: 2. Of those that a mesh axis runs over, the one named last changes fastest.
Arguments:
- trajectory: float32 [512, 8, 4096], P('tm', None, 'chan'), may hold values from -40 to 40
- initial: float32 [8, 4096], P(None, 'chan'), may hold values from -6 to 6
- drive_gate: bfloat16 [512, 8, 4096], P('tm', None, 'chan'), may hold values from -16 to 4
- drive_candidate: bfloat16 [512, 8, 4096], P('tm', None, 'chan'), may hold values from -6 to 6
- gate_weight: bfloat16 [4096, 4096], P('chan'), may hold values from -0.0234375 to 0.0234375
- candidate_weight: bfloat16 [4096, 4096], P('chan'), may hold values from -0.09375 to 0.09375
Outputs:
- newton_states: float32 [512, 8, 4096], P('tm', None, 'chan')
- residual_norm: float32 [], replicated
All inputs are finite; a program needn't handle non-finite values.
Results may differ from a plain program's by a relative error of at most 0.0016.
Values may be sent and summed in bfloat16 or wider, within the bound.
A program may use at most 128 MiB of HBM per device.

v0:
```python
import jax
import jax.numpy as jnp
from jax import lax
from jax.sharding import PartitionSpec as P


def passed_along(shard, axis, by):
    size = lax.axis_size(axis)
    pairs = [(i, i + by) for i in range(size) if 0 <= i + by < size]
    return lax.ppermute(shard, axis, pairs)


def combine_maps(earlier, later):
    return (later[0] * earlier[0], later[0] * earlier[1] + later[1])


def local(trajectory, initial, drive_gate, drive_candidate, gate_weight, candidate_weight):
    local_width = trajectory.shape[2]
    chan_index = lax.axis_index("chan")
    time_index = lax.axis_index("tm")
    final_row = trajectory[-1]
    arrived = passed_along(final_row, "tm", 1)
    before = jnp.where(time_index == 0, initial, arrived)
    previous = jnp.concatenate([before[None], trajectory[:-1]], 0)
    flat_rows = previous.reshape(-1, local_width).astype(jnp.bfloat16)
    numbers = (((0,), (1,)), ((), ()))
    gate_part = lax.dot_general(gate_weight, flat_rows, numbers, preferred_element_type=jnp.float32)
    cand_part = lax.dot_general(
        candidate_weight, flat_rows, numbers, preferred_element_type=jnp.float32
    )
    summed = lax.psum_scatter(
        jnp.stack([gate_part, cand_part], 1), "chan", scatter_dimension=0, tiled=True
    )
    gate_sum = summed[:, 0, :].T
    cand_sum = summed[:, 1, :].T
    gate_block = lax.dynamic_slice_in_dim(gate_weight, chan_index * local_width, local_width, 1)
    cand_block = lax.dynamic_slice_in_dim(
        candidate_weight, chan_index * local_width, local_width, 1
    )
    gate_diagonal = jnp.diagonal(gate_block).astype(jnp.float32)
    cand_diagonal = jnp.diagonal(cand_block).astype(jnp.float32)
    gate_pre = gate_sum.reshape(previous.shape) + drive_gate.astype(jnp.float32)
    cand_pre = cand_sum.reshape(previous.shape) + drive_candidate.astype(jnp.float32)
    update = jax.nn.sigmoid(gate_pre)
    candidate = jnp.tanh(cand_pre)
    mapped = (1.0 - update) * previous + update * candidate
    jacobian = (
        1.0
        - update
        + update * (1.0 - update) * (candidate - previous) * gate_diagonal
        + update * (1.0 - candidate * candidate) * cand_diagonal
    )
    offset = mapped - jacobian * previous
    ones_state = jnp.ones_like(initial)
    zeros_state = jnp.zeros_like(initial)
    running_product, running_state = lax.associative_scan(combine_maps, (jacobian, offset), axis=0)
    block_product = running_product[-1]
    block_state = running_state[-1]
    all_products, all_states = (
        lax.all_gather(block_product[None], "tm", axis=0, tiled=True),
        lax.all_gather(block_state[None], "tm", axis=0, tiled=True),
    )
    inclusive_product, inclusive_state = lax.associative_scan(
        combine_maps, (all_products, all_states), axis=0
    )
    earlier_index = jnp.maximum(time_index - 1, 0)
    picked_product = lax.dynamic_index_in_dim(inclusive_product, earlier_index, 0, keepdims=False)
    picked_state = lax.dynamic_index_in_dim(inclusive_state, earlier_index, 0, keepdims=False)
    prefix_product = jnp.where(time_index == 0, ones_state, picked_product)
    prefix_state = jnp.where(time_index == 0, zeros_state, picked_state)
    entry_state = prefix_product * initial + prefix_state
    newton_states = running_product * entry_state[None] + running_state
    missing = trajectory - mapped
    squared_total = lax.psum(jnp.sum(missing * missing), ("chan", "tm"))
    entries = trajectory.size * lax.axis_size("chan") * lax.axis_size("tm")
    residual_norm = jnp.sqrt(squared_total / entries + 1e-06)
    return (newton_states, residual_norm)


def solution(mesh):
    placed = (
        P("tm", None, "chan"),
        P(None, "chan"),
        P("tm", None, "chan"),
        P("tm", None, "chan"),
        P("chan", None),
        P("chan", None),
    )
    return jax.shard_map(
        local, mesh=mesh, in_specs=placed, out_specs=(P("tm", None, "chan"), P()), check_vma=False
    )
```

profile of v0, /device:TPU:0, one launch (start us, length us, event | category | flops | bytes accessed | tf_op | source)
XLA Modules:
  0.0 529.5 jit_solution(3640614017079482027)
XLA Ops:
  8.0 2.4 collective-permute-start
  12.2 7.0 %convolution_bitcast_fusion = f32[4096,1,512]{0,2,1:T(8,128)S(1)} fusion(bf16[1024,4096]{1,0:T(8,128)(2,1)} %param.11, f32[63,8,1024]{2,1,0:T(8,128)S(1)} %slice.269, f32[1,8,1024]{2,1,0:T(8,128)S(1)} %select_bitcast_fusion), kind=kOutput, calls=%fused_computation.3 | convolution fusion | flops 4295491584 | bytes 18874368 | tf_op jit(solution)/shard_map/dot_general | solution.py:28
  19.2 4.6 convolution_bitcast_fusion.1
  23.8 6.3 %pad_maximum_fusion = f32[4096,2,512]{0,2,1:T(8,128)} fusion(f32[4096,1,512]{0,2,1:T(8,128)S(1)} %convolution_bitcast_fusion, f32[4096,1,512]{0,2,1:T(8,128)S(1)} %convolution_bitcast_fusion.1), kind=kLoop, calls=%fused_computation.2 | loop fusion | flops 4194304 | bytes 33554432 | tf_op jit(solution)/shard_map/stack | solution.py:32
  30.1 4.7 constant_dynamic-slice_fusion
  34.9 16.3 %gather_fusion = bf16[1024]{0:T(1024)(128)(2,1)S(1)} fusion(bf16[1024,1024]{1,0:T(8,128)(2,1)} %get-tuple-element.47, s32[1024]{0:T(1024)S(1)} %bitcast.68), kind=kCustom, calls=%fused_computation | custom fusion | bytes 12288 | tf_op jit(solution)/shard_map/jit(diagonal)/cond/branch_0_fun/gather | solution.py:40
  51.2 15.8 %gather_fusion.1 = bf16[1024]{0:T(1024)(128)(2,1)S(1)} fusion(bf16[1024,1024]{1,0:T(8,128)(2,1)} %get-tuple-element.46, s32[1024]{0:T(1024)S(1)} %bitcast.69), kind=kCustom, calls=%fused_computation.1 | custom fusion | bytes 12288 | tf_op jit(solution)/shard_map/jit(diagonal)/cond/branch_0_fun/gather | solution.py:41
  67.1 247.4 %reduce-scatter.2.cloned.1.call-done = f32[1024,2,512]{0,2,1:T(8,128)} async-done(((f32[4096,2,512]{0,2,1:T(8,128)}), f32[1024,2,512]{0,2,1:T(8,128)}) %reduce-scatter.2.cloned.1.call-update) | async-done | bytes 4194320 | tf_op jit(solution)/shard_map/reduce_scatter | solution.py:31
  314.5 5.1 multiply_reduce_fusion
  328.1 2.0 pad.133
  330.2 2.0 pad.115
  333.6 2.0 pad.114
  343.5 3.4 pad.135
  348.5 3.4 pad.116
  351.9 1.9 pad.117
  355.6 1.9 add_multiply_fusion.5
  358.6 5.1 pad.119
  364.7 3.3 pad.118
  368.8 2.3 add_multiply_fusion.3
  373.0 5.9 %pad.139 = f32[32,8,1024]{2,1,0:T(8,128)} pad(f32[16,8,1024]{2,1,0:T(8,128)S(1)} %copy-done.15, f32[]{:T(128)} %constant.38.clone.1), padding=1_0_1x0_0_0x0_0_0 | pad | bytes 1572868 | tf_op jit(solution)/shard_map/pad | solution.py:56
  378.9 5.9 %pad.120 = f32[32,8,1024]{2,1,0:T(8,128)} pad(f32[16,8,1024]{2,1,0:T(8,128)S(1)} %pad_maximum_fusion.4, f32[]{:T(128)} %constant.38.clone.1), padding=0_1_1x0_0_0x0_0_0 | pad | bytes 1572868 | tf_op jit(solution)/shard_map/pad | solution.py:56
  384.8 9.2 %pad.121 = f32[32,8,1024]{2,1,0:T(8,128)} pad(f32[16,8,1024]{2,1,0:T(8,128)} %add.228, f32[]{:T(128)} %constant.38.clone.1), padding=1_0_1x0_0_0x0_0_0 | pad | bytes 1572868 | tf_op jit(solution)/shard_map/pad | solution.py:56
  393.9 2.5 add.249
  396.4 3.6 add_multiply_fusion.1
  401.1 12.4 %pad.141 = f32[64,8,1024]{2,1,0:T(8,128)S(1)} pad(f32[32,8,1024]{2,1,0:T(8,128)} %add.249, f32[]{:T(128)} %constant.38.clone.1), padding=1_0_1x0_0_0x0_0_0 | pad | bytes 3145732 | tf_op jit(solution)/shard_map/pad | solution.py:56
  414.6 16.6 %pad.140 = f32[64,8,1024]{2,1,0:T(8,128)} pad(f32[32,8,1024]{2,1,0:T(8,128)} %pad_maximum_fusion.3, f32[]{:T(128)} %constant.38.clone.1), padding=0_1_1x0_0_0x0_0_0 | pad | bytes 3145732 | tf_op jit(solution)/shard_map/pad | solution.py:56
  432.0 9.2 %all_gather.7 = f32[8,8,1024]{2,1,0:T(8,128)S(1)} all-gather(f32[1,8,1024]{2,1,0:T(8,128)S(1)} %slice_add_fusion.8), channel_id=1, replica_groups=mesh['chan'=4,'tm'=8] {'tm'}, dimensions={0}, use_global_device_ids=true | all-gather | bytes 294912 | tf_op jit(solution)/shard_map/all_gather | solution.py:61
  441.2 11.0 %pad.123 = f32[64,8,1024]{2,1,0:T(8,128)} pad(f32[32,8,1024]{2,1,0:T(8,128)S(1)} %copy-done.11, f32[]{:T(128)} %constant.38.clone.1), padding=1_0_1x0_0_0x0_0_0 | pad | bytes 3145732 | tf_op jit(solution)/shard_map/pad | solution.py:56
  453.5 11.1 %pad.122 = f32[64,8,1024]{2,1,0:T(8,128)} pad(f32[32,8,1024]{2,1,0:T(8,128)S(1)} %pad_maximum_fusion.2, f32[]{:T(128)} %constant.38.clone.1), padding=0_1_1x0_0_0x0_0_0 | pad | bytes 3145732 | tf_op jit(solution)/shard_map/pad | solution.py:56
  465.3 9.2 %all_gather.6 = f32[8,8,1024]{2,1,0:T(8,128)S(1)} all-gather(f32[1,8,1024]{2,1,0:T(8,128)S(1)} %slice_add_fusion.10), channel_id=1, replica_groups=mesh['chan'=4,'tm'=8] {'tm'}, dimensions={0}, use_global_device_ids=true | all-gather | bytes 294912 | tf_op jit(solution)/shard_map/all_gather | solution.py:60
  475.6 5.2 multiply_add_fusion
  480.8 40.1 %psum.7 = f32[]{:T(128)} all-reduce(f32[]{:T(128)} %get-tuple-element.2), channel_id=1, replica_groups=mesh['chan'=4,'tm'=8] {'chan','tm'}, use_global_device_ids=true, to_apply=%region_2.3 | all-reduce | flops 1 | bytes 8 | tf_op jit(solution)/shard_map/psum | solution.py:74
  (122 shorter events, 34.2 us)
Async XLA Ops:
  7.2 5.0 copy-start.21
  7.2 307.3 %reduce-scatter.2.cloned.1.call-start = ((), (), s32[]{:S(2)}) async-start(), calls=%async_computation.1 | async-start | bytes 20971520 | tf_op jit(solution)/shard_map/reduce_scatter | solution.py:31
  8.0 4.1 collective-permute-start
  12.1 7.1 %copy-start.19 = (bf16[1024,4096]{1,0:T(8,128)(2,1)S(1)}, bf16[1024,4096]{1,0:T(8,128)(2,1)}, u32[]{:S(2)}) copy-start(bf16[1024,4096]{1,0:T(8,128)(2,1)} %param.10) | copy-start | bytes 25165828
  34.8 279.6 %copy-start.9 = (bf16[64,8,1024]{2,1,0:T(8,128)(2,1)S(1)}, bf16[64,8,1024]{2,1,0:T(8,128)(2,1)}, u32[]{:S(2)}) copy-start(bf16[64,8,1024]{2,1,0:T(8,128)(2,1)} %param.9) | copy-start | bytes 3145732
  314.5 5.1 copy-start
  314.5 5.1 copy-start.10
  321.2 1.3 copy-start.1
  321.2 2.0 copy-start.3
  323.5 2.0 copy-start.17
  353.8 3.7 copy-start.13
  353.8 3.7 copy-start.14
  353.8 4.4 copy-start.20
  357.5 1.0 copy-start.18
  368.8 2.3 copy-start.7
  368.8 2.3 copy-start.8
  371.1 1.9 copy-start.15
  372.7 6.1 %copy-start.16 = (f32[15,8,1024]{2,1,0:T(8,128)S(1)}, f32[15,8,1024]{2,1,0:T(8,128)}, u32[]{:S(2)}) copy-start(f32[15,8,1024]{2,1,0:T(8,128)} %get-tuple-element.10) | copy-start | bytes 1474564
  384.8 11.7 %copy-start.2 = (f32[64,8,1024]{2,1,0:T(8,128)S(1)}, f32[64,8,1024]{2,1,0:T(8,128)}, u32[]{:S(2)}) copy-start(f32[64,8,1024]{2,1,0:T(8,128)} %copy-done.1) | copy-start | bytes 6291460
  393.9 2.5 copy-start.4
  393.9 2.5 copy-start.5
  396.4 3.6 copy-start.6
  401.1 12.4 %copy-start.12 = (f32[31,8,1024]{2,1,0:T(8,128)S(1)}, f32[31,8,1024]{2,1,0:T(8,128)}, u32[]{:S(2)}) copy-start(f32[31,8,1024]{2,1,0:T(8,128)} %get-tuple-element.7) | copy-start | bytes 3047428
  414.6 26.6 %copy-start.11 = (f32[32,8,1024]{2,1,0:T(8,128)S(1)}, f32[32,8,1024]{2,1,0:T(8,128)}, u32[]{:S(2)}) copy-start(f32[32,8,1024]{2,1,0:T(8,128)} %add.229) | copy-start | bytes 3145732
  474.8 0.8 copy-start.22
Sparse Core Ops, SparseCore 0:
  30.2 284.2 reduce-scatter.1
where the time goes:
time: 536 us; the launch traced here: 530 us
  waiting for transfers between devices  247 us (46%)
  local copies, waits for them, and re-layouts  142 us (26%)
  blocking collectives  58.6 us (11%)
  other arithmetic  50.7 us (9%)
  between operations  16.4 us (3%)
  matrix products  11.6 us (2%)
    reduce_scatter x1, waiting for transfers between devices, local(): lax.psum_scatter(jnp.stack([gate_part, cand_part], 1), 'chan', scatter_di...  247 us
    pad x20, local copies, waits for them, and re-layouts, local(): lax.associative_scan(combine_maps, (jacobian, offset), axis=0)  98 us
    psum x1, blocking collectives, local(): squared_total = lax.psum(jnp.sum(missing * missing), ('chan', 'tm'))  40.1 us
    gather x1, local copies, waits for them, and re-layouts, local(): gate_diagonal = jnp.diagonal(gate_block).astype(jnp.float32)  16.3 us
    gather x1, local copies, waits for them, and re-layouts, local(): cand_diagonal = jnp.diagonal(cand_block).astype(jnp.float32)  15.8 us
    add x12, other arithmetic, local(): lax.associative_scan(combine_maps, (jacobian, offset), axis=0)  13.1 us
  transfers between devices with their start and end apart: 2, of which 1 were waited for; matrix products, arithmetic and copies ran while one was open for 7% of the time, Pallas kernels for 0%

commit v1 on v0

v1 whole, which is shorter than its diff:
```python
import functools

import jax
import jax.numpy as jnp
from jax import lax
from jax.experimental import pallas as pl
from jax.experimental.pallas import tpu as pltpu
from jax.sharding import PartitionSpec as P

MESH = pl.DeviceIdType.MESH
BF16 = jnp.bfloat16
F32 = jnp.float32


def kernel(
    nz, nt, chunks, tile,
    traj, init, drive_g, drive_c, gate_w, cand_w,
    out, total,
    wbuf, abuf, prev0, diag, prod, carry, ssq, partner_map, maps, tsums, zsums,
    local_sem, wz_send, wz_recv, wx_send, wx_recv, wc_send, wc_recv,
    a_send, a_recv, row_sem, pm_sem, m_send, m_recv, ts_send, ts_recv, zs_send, zs_recv,
):
    z = lax.axis_index("chan")
    t = lax.axis_index("tm")
    steps, batch, width = traj.shape
    nc = nt // 2
    chip = lax.div(t, 2)
    core = lax.rem(t, 2)
    partner = (z, t + 1 - 2 * core)
    part = width // nt
    weights = (gate_w, cand_w)
    rows = steps * batch // chunks
    chunk_steps = steps // chunks

    def remote(src, dst, send, recv, device):
        return pltpu.make_async_remote_copy(
            src_ref=src, dst_ref=dst, send_sem=send, recv_sem=recv,
            device_id=device, device_id_type=MESH,
        )

    def zmod(v):
        return lax.rem(v + 2 * nz, nz)

    def cmod(v):
        return lax.rem(v + 2 * nc, nc)

    def wslot(g, source, p):
        return wbuf.at[g, pl.ds(pl.multiple_of(source * width + p * part, 16), part), :]

    barrier = pltpu.get_barrier_semaphore()
    for d in range(1, nz):
        pl.semaphore_signal(barrier, inc=1, device_id=(zmod(z + d), t), device_id_type=MESH)
    for d in range(1, nt):
        pl.semaphore_signal(barrier, inc=1, device_id=(z, lax.rem(t + d, nt)), device_id_type=MESH)
    pl.semaphore_wait(barrier, nz - 1 + nt - 1)

    sent = []

    def row_copy():
        return remote(traj.at[steps - 1], prev0, row_sem.at[0], row_sem.at[1], (z, lax.rem(t + 1, nt)))

    row_copy().start()

    def z_copy(d, g):
        other = zmod(z + d)
        src = weights[g].at[
            pl.ds(pl.multiple_of(t * part, 16), part), pl.ds(pl.multiple_of(other * width, 128), width)
        ]
        return remote(src, wslot(g, z, t), wz_send.at[g, d - 1], wz_recv.at[g, d - 1], (other, t))

    for d in range(1, nz):
        for g in range(2):
            z_copy(d, g).start()

    def own_copy(g):
        return pltpu.make_async_copy(
            weights[g].at[:, pl.ds(pl.multiple_of(z * width, 128), width)],
            wbuf.at[g, pl.ds(pl.multiple_of(z * width, 128), width), :],
            local_sem.at[g],
        )

    for g in range(2):
        own_copy(g).start()

    own_columns = pl.ds(pl.multiple_of(z * width, 128), width)

    @pl.loop(1, steps // 2)
    def _(j):
        pair = traj[pl.ds(2 * j - 1, 2)].reshape(2 * batch, width)
        abuf[pl.ds(pl.multiple_of(j * 2 * batch, 16), 2 * batch), own_columns] = pair.astype(BF16)

    row_copy().wait()

    @pl.when(t == 0)
    def _():
        prev0[...] = init[...]

    first = jnp.concatenate([prev0[...], traj[0]], 0)
    abuf[pl.ds(0, 2 * batch), own_columns] = first.astype(BF16)

    def a_copy(direction, source, i):
        slot = abuf.at[pl.ds(i * rows, rows), pl.ds(pl.multiple_of(source * width, 128), width)]
        to = z + 1 if direction == 0 else z - 1
        return remote(slot, slot, a_send.at[direction, source, i], a_recv.at[source, i], (to, t))

    for i in range(chunks):
        @pl.when(z < nz - 1)
        def _():
            a_copy(0, z, i).start()

        @pl.when(z > 0)
        def _():
            a_copy(1, z, i).start()

    for g in range(2):
        own_copy(g).wait()
        for j in range(width // 128):
            block = wbuf[g, pl.ds(pl.multiple_of(z * width + j * 128, 128), 128), pl.ds(j * 128, 128)]
            eye = lax.broadcasted_iota(jnp.int32, (128, 128), 0) == lax.broadcasted_iota(
                jnp.int32, (128, 128), 1
            )
            line = jnp.sum(jnp.where(eye, block.astype(F32), 0.0), axis=0, keepdims=True)
            diag[g, :, pl.ds(j * 128, 128)] = jnp.broadcast_to(line, (batch, 128))

    carry[0] = jnp.ones((batch, width), F32)
    carry[1] = jnp.zeros((batch, width), F32)
    ssq[...] = jnp.zeros((batch, width), F32)

    def x_copy(d, g, dq):
        slot = wslot(g, zmod(z - d), t)
        return remote(
            slot, slot, wx_send.at[g, d - 1, dq - 1], wx_recv.at[g, d - 1, dq - 1],
            (z, 2 * cmod(chip + dq) + core),
        )

    def c_copy(d, g, dq, side):
        slot = wslot(g, zmod(z - d), 2 * cmod(chip - dq) + side)
        return remote(slot, slot, wc_send.at[g, d - 1, dq], wc_recv.at[g, d - 1, dq], partner)

    def x_arrival(d, g, dq):
        slot = wslot(g, zmod(z - d), 2 * cmod(chip - dq) + core)
        return remote(slot, slot, wx_send.at[g, d - 1, dq - 1], wx_recv.at[g, d - 1, dq - 1], partner)

    def z_arrival(d, g):
        slot = wslot(g, zmod(z - d), t)
        return remote(slot, slot, wz_send.at[g, d - 1], wz_recv.at[g, d - 1], partner)

    for d in range(1, nz):
        for g in range(2):
            z_arrival(d, g).wait_recv()
            for dq in range(1, nc):
                x_copy(d, g, dq).start()
            c_copy(d, g, 0, core).start()

    onward = [(d, g, dq) for d in range(1, nz) for g in range(2) for dq in range(1, nc)]

    def relay(d, i):
        @pl.when(z - d >= 0)
        def _():
            a_copy(0, z - d, i).wait_recv()

            @pl.when(z < nz - 1)
            def _():
                a_copy(0, z - d, i).start()

        @pl.when(z + d < nz)
        def _():
            a_copy(1, z + d, i).wait_recv()

            @pl.when(z > 0)
            def _():
                a_copy(1, z + d, i).start()

    early = [(d, i) for d in range(1, nz - 1) for i in range(chunks)]
    spread = max(1, (3 * len(early)) // 4)
    per = -(-len(onward) // spread)
    for n, (d, i) in enumerate(early):
        relay(d, i)
        for item in onward[n * per : (n + 1) * per]:
            x_arrival(*item).wait_recv()
            c_copy(*item, core).start()
    for d in range(1, nz):
        for g in range(2):
            for dq in range(nc):
                c_copy(d, g, dq, 1 - core).wait_recv()

    def compute(i):
        @pl.loop(0, width // tile)
        def _(n):
            cols = pl.ds(pl.multiple_of(n * tile, tile), tile)
            lhs = abuf[pl.ds(i * rows, rows), :]
            shape = (chunk_steps, batch, tile)
            span = pl.ds(i * chunk_steps, chunk_steps)
            gate_pre = jnp.dot(lhs, wbuf[0, :, cols], preferred_element_type=F32).reshape(shape)
            cand_pre = jnp.dot(lhs, wbuf[1, :, cols], preferred_element_type=F32).reshape(shape)
            gate_pre = gate_pre + drive_g[span, :, cols].astype(F32)
            cand_pre = cand_pre + drive_c[span, :, cols].astype(F32)
            guess = traj[span, :, cols]
            if i == 0:
                previous = jnp.concatenate([prev0[:, cols][None], guess[:-1]], 0)
            else:
                previous = traj[pl.ds(i * chunk_steps - 1, chunk_steps), :, cols]
            update = jax.nn.sigmoid(gate_pre)
            candidate = jnp.tanh(cand_pre)
            keep = 1.0 - update
            mapped = keep * previous + update * candidate
            jacobian = (
                keep
                + update * keep * (candidate - previous) * diag[0, :, cols][None]
                + update * (1.0 - candidate * candidate) * diag[1, :, cols][None]
            )
            offset = mapped - jacobian * previous
            missing = guess - mapped
            ssq[:, cols] += jnp.sum(missing * missing, axis=0)
            product = carry[0, :, cols]
            state = carry[1, :, cols]
            for s in range(chunk_steps):
                product = jacobian[s] * product
                state = jacobian[s] * state + offset[s]
                prod[i * chunk_steps + s, :, cols] = product
                out[i * chunk_steps + s, :, cols] = state
            carry[0, :, cols] = product
            carry[1, :, cols] = state

    for i in range(chunks):
        relay(nz - 1, i)
        compute(i)

    def pm_copy():
        return remote(carry, partner_map, pm_sem.at[0], pm_sem.at[1], partner)

    pm_copy().start()
    mine = ssq[:, pl.ds(0, 128)]
    for j in range(1, width // 128):
        mine = mine + ssq[:, pl.ds(j * 128, 128)]
    tsums[t] = mine

    def ts_copy(d):
        slot = tsums.at[t]
        return remote(slot, slot, ts_send.at[d - 1], ts_recv.at[d - 1], (z, lax.rem(t + d, nt)))

    def ts_arrival(d):
        slot = tsums.at[lax.rem(t + nt - d, nt)]
        return remote(slot, slot, ts_send.at[d - 1], ts_recv.at[d - 1], partner)

    for d in range(1, nt):
        ts_copy(d).start()

    def m_copy(dq):
        slot = maps.at[chip]
        return remote(
            slot, slot, m_send.at[dq - 1], m_recv.at[dq - 1], (z, 2 * cmod(chip + dq) + core)
        )

    def m_arrival(dq):
        slot = maps.at[cmod(chip - dq)]
        return remote(slot, slot, m_send.at[dq - 1], m_recv.at[dq - 1], partner)

    pm_copy().wait()
    is_second = core == 1
    p_mine, s_mine, p_other, s_other = carry[0], carry[1], partner_map[0], partner_map[1]
    p_late = jnp.where(is_second, p_mine, p_other)
    s_early = jnp.where(is_second, s_other, s_mine)
    s_late = jnp.where(is_second, s_mine, s_other)
    maps[chip, 0] = p_mine * p_other
    maps[chip, 1] = p_late * s_early + s_late
    for dq in range(1, nc):
        m_copy(dq).start()

    for d in range(1, nt):
        ts_arrival(d).wait_recv()
    plane = tsums[0]
    for k in range(1, nt):
        plane = plane + tsums[k]
    zsums[z] = plane

    def zs_copy(d):
        slot = zsums.at[z]
        return remote(slot, slot, zs_send.at[d - 1], zs_recv.at[d - 1], (zmod(z + d), t))

    def zs_arrival(d):
        slot = zsums.at[zmod(z - d)]
        return remote(slot, slot, zs_send.at[d - 1], zs_recv.at[d - 1], partner)

    for d in range(1, nz):
        zs_copy(d).start()

    for dq in range(1, nc):
        m_arrival(dq).wait_recv()
    entry = init[...]
    for q in range(nc):
        entry = jnp.where(q < chip, maps[q, 0] * entry + maps[q, 1], entry)
    entry = jnp.where(is_second, p_other * entry + s_other, entry)
    carry_entry = entry
    prev0[...] = carry_entry

    @pl.loop(0, steps)
    def _(s):
        out[s] = prod[s] * prev0[...] + out[s]

    for d in range(1, nz):
        zs_arrival(d).wait_recv()
    whole = zsums[0]
    for k in range(1, nz):
        whole = whole + zsums[k]
    total[...] = whole

    for d in range(1, nz):
        zs_copy(d).wait_send()
        for g in range(2):
            z_copy(d, g).wait_send()
            for dq in range(1, nc):
                x_copy(d, g, dq).wait_send()
            for dq in range(nc):
                c_copy(d, g, dq, core).wait_send()
    for d in range(1, nt):
        ts_copy(d).wait_send()
    for dq in range(1, nc):
        m_copy(dq).wait_send()
    for i in range(chunks):
        for source in range(nz):
            @pl.when(jnp.logical_and(source <= z, z < nz - 1))
            def _():
                a_copy(0, source, i).wait_send()

            @pl.when(jnp.logical_and(source >= z, z > 0))
            def _():
                a_copy(1, source, i).wait_send()


def local(nz, nt, trajectory, initial, drive_gate, drive_candidate, gate_weight, candidate_weight):
    steps, batch, width = trajectory.shape
    nc = nt // 2
    full = gate_weight.shape[1]
    chunks = 4
    tile = min(256, width)
    dma = pltpu.SemaphoreType.DMA
    vmem = pl.BlockSpec(memory_space=pltpu.VMEM)
    hbm = pl.BlockSpec(memory_space=pl.ANY)
    states, total = pl.pallas_call(
        functools.partial(kernel, nz, nt, chunks, tile),
        out_shape=(
            jax.ShapeDtypeStruct((steps, batch, width), F32),
            jax.ShapeDtypeStruct((batch, 128), F32),
        ),
        in_specs=[vmem, vmem, vmem, vmem, hbm, hbm],
        out_specs=(vmem, vmem),
        scratch_shapes=[
            pltpu.VMEM((2, full, width), BF16),
            pltpu.VMEM((steps * batch, full), BF16),
            pltpu.VMEM((batch, width), F32),
            pltpu.VMEM((2, batch, width), F32),
            pltpu.VMEM((steps, batch, width), F32),
            pltpu.VMEM((2, batch, width), F32),
            pltpu.VMEM((batch, width), F32),
            pltpu.VMEM((2, batch, width), F32),
            pltpu.VMEM((nc, 2, batch, width), F32),
            pltpu.VMEM((nt, batch, 128), F32),
            pltpu.VMEM((nz, batch, 128), F32),
            dma((2,)),
            dma((2, nz - 1)),
            dma((2, nz - 1)),
            dma((2, nz - 1, nc - 1)),
            dma((2, nz - 1, nc - 1)),
            dma((2, nz - 1, nc)),
            dma((2, nz - 1, nc)),
            dma((2, nz, chunks)),
            dma((nz, chunks)),
            dma((2,)),
            dma((2,)),
            dma((nc - 1,)),
            dma((nc - 1,)),
            dma((nt - 1,)),
            dma((nt - 1,)),
            dma((nz - 1,)),
            dma((nz - 1,)),
        ],
        compiler_params=pltpu.CompilerParams(
            collective_id=0, has_side_effects=True, vmem_limit_bytes=56 * 2**20
        ),
    )(trajectory, initial, drive_gate, drive_candidate, gate_weight, candidate_weight)
    entries = trajectory.size * nz * nt
    residual_norm = jnp.sqrt(jnp.sum(total) / entries + 1e-06)
    return (states, residual_norm)


def solution(mesh):
    placed = (
        P("tm", None, "chan"),
        P(None, "chan"),
        P("tm", None, "chan"),
        P("tm", None, "chan"),
        P("chan", None),
        P("chan", None),
    )
    body = functools.partial(local, mesh.shape["chan"], mesh.shape["tm"])
    return jax.shard_map(
        body, mesh=mesh, in_specs=placed, out_specs=(P("tm", None, "chan"), P()), check_vma=False
    )
```

time: 536 us -> 130 us (0.24); the launches traced: 530 us -> 130 us
  waiting for transfers between devices: 247 us -> 0 us
  local copies, waits for them, and re-layouts: 142 us -> 3.16 us
  Pallas kernels: 0 us -> 123 us
  blocking collectives: 58.6 us -> 0 us
  other arithmetic: 50.7 us -> 1.29 us
  between operations: 16.4 us -> 2.46 us
  matrix products: 11.6 us -> 0 us
    reduce_scatter x1 -> x0, waiting for transfers between devices: 247 us -> none  [local(): lax.psum_scatter(jnp.stack([gate_part, cand_part], 1), 'chan', scatter_di...]
    pallas_call x0 -> x1, Pallas kernels: none -> 123 us  [local(): pl.pallas_call(functools.partial(kernel, nz, nt, chunks, tile), out_shape...]
    pad x28 -> x0, local copies, waits for them, and re-layouts: 98.2 us -> none  [the longest x20 98 us: local(): lax.associative_scan(combine_maps, (jacobian, offset), axis=0)]
    psum x1 -> x0, blocking collectives: 40.1 us -> none  [local(): squared_total = lax.psum(jnp.sum(missing * missing), ('chan', 'tm'))]
    gather x2 -> x0, local copies, waits for them, and re-layouts: 32.2 us -> none  [the longest x1 16.3 us: local(): gate_diagonal = jnp.diagonal(gate_block).astype(jnp.float32)]
    all_gather x2 -> x0, blocking collectives: 18.5 us -> none  [the longest x1 9.25 us: local(): lax.all_gather(block_state[None], 'tm', axis=0, tiled=True)]
    add x18 -> x0, other arithmetic: 18.4 us -> none  [the longest x12 13.1 us: local(): lax.associative_scan(combine_maps, (jacobian, offset), axis=0)]
    dot_general x2 -> x0, matrix products: 11.6 us -> none  [the longest x1 7.05 us: local(): lax.dot_general(candidate_weight, flat_rows, numbers, preferred_element_t...]
  transfers between devices with their start and end apart: 2 -> 0, of which waited for: 1 -> 0; matrix products, arithmetic and copies ran while one was open for 7% -> 0% of each run, Pallas kernels for 0% -> 0%
where the time goes in v1:
time: 130 us
  Pallas kernels  123 us (95%)
  local copies, waits for them, and re-layouts  3.16 us (2%)
  between operations  2.46 us (2%)
    pallas_call x1, Pallas kernels, local(): pl.pallas_call(functools.partial(kernel, nz, nt, chunks, tile), out_shape...  123 us
    unnamed x1, local copies, waits for them, and re-layouts  3.16 us

profile of v1, /device:TPU:0, one launch (start us, length us, event | category | flops | bytes accessed | tf_op | source)
XLA Modules:
  0.0 130.2 jit_solution(759785471120313028)
XLA Ops:
  0.6 123.3 %shard_map.77 = (f32[64,8,1024]{2,1,0:T(8,128)}, f32[8,128]{1,0:T(8,128)}) custom-call(f32[64,8,1024]{2,1,0:T(8,128)} %traj.1, f32[8,1024]{1,0:T(8,128)} %init.1, bf16[64,8,1024]{2,1,0:T(8,128)(2,1)} %drive_g.1, bf16[64,8,1024]{2,1,0:T(8,128)(2,1)} %drive_c.1, bf16[1024,4096]{1,0:T(8,128)(2,1)} %gate_w.1, bf16[1024,4096]{1,0:T(8,128)(2,1)} %cand_w.1), custom_call_target="tpu_custom_call" | custom-call | tf_op jit(solution)/shard_map/pallas_call | solution.py:340
  123.9 1.3 reduce_sum.9
  125.9 3.2 %copy.9 = f32[64,8,1024]{2,1,0:T(8,128)} copy(f32[64,8,1024]{2,1,0:T(8,128)} %get-tuple-element.8) | data formatting | bytes 4194304
